TPU v7x, 32 devices: a whole 2x2x4 slice. The times are simulated.
32 devices in a mesh: tgt: 8 (over y, x, core), src: 4 (over z).
Axes of the slice: x: 2, y: 2, z: 4, core: 2. Of those that a mesh axis runs over, the one named last changes fastest.
Arguments:
- fibre_points: float32 [3, 64, 64], P(None, ('tgt', 'src')), may hold values from -6 to 6
- shell_points: float32 [3, 128, 64], P(None, 'tgt', 'src'), may hold values from -7 to 7, as said below
- bending: float32 [64, 64], replicated, may hold values from -0.12 to 0.12
- shell_inverse: bfloat16 [3, 128, 64, 3, 64, 128], P(None, 'tgt', None, None, 'src'), may hold values from -0.0390625 to 0.0390625
Outputs:
- fibre_velocity: float32 [3, 64, 64], P(None, ('tgt', 'src'))
- shell_density: float32 [3, 128, 64], P(None, 'tgt', 'src')
Inputs may be any that keep to these rules, and one draw needn't show every extreme that they name: `shell_points`: every shell node lies on the sphere of radius 7 about the anchor.
All inputs are finite; a program needn't handle non-finite values.
Results may differ from a plain program's by a relative error of at most 0.0029.
Values may be sent and summed in bfloat16 or wider, within the bound.
A program may use at most 64 MiB of HBM per device.

v0:
```python
import math

import jax
import jax.numpy as jnp
from jax import lax
from jax.sharding import PartitionSpec as P

mobility = 1.0 / (8.0 * math.pi)
soften_sq = 0.0025


def stokes_flow(targets, sources, strength):
    delta_x = targets[0][:, None] - sources[0][None, :]
    delta_y = targets[1][:, None] - sources[1][None, :]
    delta_z = targets[2][:, None] - sources[2][None, :]
    dist_sq = delta_x * delta_x + delta_y * delta_y + delta_z * delta_z
    inv_root = lax.rsqrt(dist_sq + soften_sq)
    inv_cubed = inv_root * inv_root * inv_root
    projection = (
        delta_x * strength[0][None, :]
        + delta_y * strength[1][None, :]
        + delta_z * strength[2][None, :]
    ) * inv_cubed
    diagonal_part = (dist_sq + 2.0 * soften_sq) * inv_cubed
    flow_x = jnp.sum(diagonal_part * strength[0][None, :] + projection * delta_x, axis=1)
    flow_y = jnp.sum(diagonal_part * strength[1][None, :] + projection * delta_y, axis=1)
    flow_z = jnp.sum(diagonal_part * strength[2][None, :] + projection * delta_z, axis=1)
    return mobility * jnp.stack([flow_x, flow_y, flow_z])


def block_width(column_count, target_count):
    widest = 128
    while widest * 2 * target_count <= 1 << 20:
        widest = widest * 2
    return math.gcd(column_count, widest)


def source_sum(running, targets, places, pushes):
    block_size = block_width(places.shape[1], targets.shape[1])
    turns = places.shape[1] // block_size

    def add_block(counter, partial_value):
        offset = counter * block_size
        part_places = lax.dynamic_slice_in_dim(places, offset, block_size, 1)
        part_pushes = lax.dynamic_slice_in_dim(pushes, offset, block_size, 1)
        return partial_value + stokes_flow(targets, part_places, part_pushes)

    return lax.fori_loop(0, turns, add_block, running)


def fibre_fold(targets, running, pieces):
    return source_sum(running, targets, pieces[0].reshape(3, -1), pieces[1].reshape(3, -1))


def per_device(fibre_points, shell_points, bending, shell_inverse):
    shell_rows = lax.all_gather(shell_points, "src", axis=2, tiled=True)
    columns_pos = lax.all_gather(shell_points, "tgt", axis=1, tiled=True)
    forces = -jnp.einsum("cfm,nm->cfn", fibre_points, bending, precision=lax.Precision.HIGHEST)
    fibre_block = lax.all_gather(fibre_points, "src", axis=1, tiled=True)
    block_flat = fibre_block.reshape(3, -1)
    targets = jnp.concatenate([block_flat, shell_rows.reshape(3, -1)], axis=1)
    zeros_flow = jnp.zeros(targets.shape, jnp.float32)
    flow_all = fibre_fold(
        targets,
        zeros_flow,
        (
            lax.all_gather(fibre_points, "tgt", axis=1, tiled=True),
            lax.all_gather(forces, "tgt", axis=1, tiled=True),
        ),
    )
    block_count = block_flat.shape[1]
    fibre_part = flow_all[:, :block_count].reshape(fibre_block.shape)
    shell_part = flow_all[:, block_count:].reshape(shell_rows.shape)
    fibre_flow = lax.psum_scatter(fibre_part, "src", scatter_dimension=1, tiled=True)
    shell_flow = lax.psum_scatter(shell_part, "src", scatter_dimension=2, tiled=True)
    columns = lax.all_gather(shell_flow.astype(jnp.bfloat16), "tgt", axis=1, tiled=True)
    density_rows = -jnp.einsum(
        "xaqcbn,cnb->xaq", shell_inverse, columns, preferred_element_type=jnp.float32
    )
    density = lax.psum_scatter(density_rows, "src", scatter_dimension=2, tiled=True)
    column_density = lax.all_gather(density, "tgt", axis=1, tiled=True)
    zeros_back = jnp.zeros(block_flat.shape, jnp.float32)
    back_block = source_sum(
        zeros_back, block_flat, columns_pos.reshape(3, -1), column_density.reshape(3, -1)
    )
    shell_back = lax.psum_scatter(
        back_block.reshape(fibre_block.shape), "src", scatter_dimension=1, tiled=True
    )
    velocity = fibre_flow + shell_back
    return (velocity, density)


def solution(mesh):
    placed = (
        P(None, ("tgt", "src"), None),
        P(None, "tgt", "src"),
        P(),
        P(None, "tgt", None, None, "src", None),
    )
    return jax.shard_map(
        per_device,
        mesh=mesh,
        in_specs=placed,
        out_specs=(P(None, ("tgt", "src"), None), P(None, "tgt", "src")),
        check_vma=False,
    )
```

profile of v0, /device:TPU:0, one launch (start us, length us, event | category | flops | bytes accessed | tf_op | source)
XLA Modules:
  0.0 174.0 jit_solution(9149982009309895691)
XLA Ops:
  7.2 0.7 copy.22
  7.9 14.9 %all_gather.21 = f32[3,8,64]{2,0,1:T(4,128)S(1)} all-gather(f32[3,2,64]{2,0,1:T(4,128)S(1)} %copy.22), channel_id=1, replica_groups=mesh['tgt'=8,'src'=4] {'src'}, dimensions={1}, use_global_device_ids=true | all-gather | bytes 7680 | tf_op jit(solution)/shard_map/all_gather | solution.py:59
  22.8 9.1 %all_gather.23 = f32[3,16,64]{2,0,1:T(4,128)S(1)} all-gather(f32[3,2,64]{2,0,1:T(4,128)S(1)} %copy.22), channel_id=1, replica_groups=mesh['tgt'=8,'src'=4] {'tgt'}, dimensions={1}, use_global_device_ids=true | all-gather | bytes 13824 | tf_op jit(solution)/shard_map/all_gather | solution.py:67
  31.9 0.8 convolution_negate_fusion
  32.8 0.1 reshape.55
  32.9 0.1 reshape.57
  33.0 9.1 %all_gather.24 = f32[3,16,64]{2,0,1:T(4,128)S(1)} all-gather(f32[3,2,64]{2,0,1:T(4,128)S(1)} %convolution_negate_fusion), channel_id=1, replica_groups=mesh['tgt'=8,'src'=4] {'tgt'}, dimensions={1}, use_global_device_ids=true | all-gather | bytes 13824 | tf_op jit(solution)/shard_map/all_gather | solution.py:68
  42.0 0.1 reshape.58
  42.1 0.8 copy.24
  42.9 13.3 %all_gather.22 = f32[3,16,64]{1,0,2:T(4,128)S(1)} all-gather(f32[3,16,16]{1,0,2:T(4,128)S(1)} %copy.24), channel_id=1, replica_groups=mesh['tgt'=8,'src'=4] {'src'}, dimensions={2}, use_global_device_ids=true | all-gather | bytes 15360 | tf_op jit(solution)/shard_map/all_gather | solution.py:56
  56.3 0.1 copy.25
  56.4 0.1 reshape.56
  56.5 10.0 %while.9 = (s32[]{:T(128)}, f32[3,1536]{1,0:T(4,128)S(1)}, f32[3,1536]{1,0:T(4,128)S(1)}, f32[3,1024]{1,0:T(4,128)S(1)}, f32[3,1024]{1,0:T(4,128)S(1)}, /*index=...) while((s32[]{:T(128)}, f32[3,1536]{1,0:T(4,128)S(1)}, ...), condition=%wide.region_4.0_spmd.clone, body=%wide.region_0.0_spmd.clone.sunk | while | flops 24397832 | bytes 202961 | solution.py:48
  56.5 0.1 fusion.44
  56.7 4.7 %fusion.45 = (f32[1536]{0:T(1024)S(1)}, f32[1536]{0:T(1024)S(1)}, f32[1536]{0:T(1024)S(1)}) fusion(f32[512]{0:T(512)S(1)} %bitcast.39, f32[512]{0:T(512)S(1)} %bitcast.42, f32[1536]{0:T(1024)S(1)} %get-tuple-element.215, f32[512]{0:T(512)S(1)} %bitcast.41, f32[1536]{0:T(1024)S(1)} %get-tuple-element.217, f32[512]{0:T(512)S(1)} %bitcast.43, ...), kind=kLoop, calls=%fused_computation.16.clone.1 | loop fusion | flops 24374784 | bytes 49152 | tf_op jit(solution)/shard_map/while/body/eval_jaxpr/reduce_sum | solution.py:25
  61.5 0.1 fusion.44
  61.7 4.7 %fusion.45 = (f32[1536]{0:T(1024)S(1)}, f32[1536]{0:T(1024)S(1)}, f32[1536]{0:T(1024)S(1)}) fusion(f32[512]{0:T(512)S(1)} %bitcast.39, f32[512]{0:T(512)S(1)} %bitcast.42, f32[1536]{0:T(1024)S(1)} %get-tuple-element.215, f32[512]{0:T(512)S(1)} %bitcast.41, f32[1536]{0:T(1024)S(1)} %get-tuple-element.217, f32[512]{0:T(512)S(1)} %bitcast.43, ...), kind=kLoop, calls=%fused_computation.16.clone.1 | loop fusion | flops 24374784 | bytes 49152 | tf_op jit(solution)/shard_map/while/body/eval_jaxpr/reduce_sum | solution.py:25
  66.5 0.1 reshape.60
  66.6 0.1 copy.33
  66.7 0.7 reshape.64
  67.5 8.3 %all_gather.25 = f32[3,128,16]{2,1,0:T(8,128)S(1)} all-gather(f32[3,16,16]{2,1,0:T(8,128)S(1)} %copy-done.1), channel_id=1, replica_groups=mesh['tgt'=8,'src'=4] {'tgt'}, dimensions={1}, use_global_device_ids=true | all-gather | bytes 27648 | tf_op jit(solution)/shard_map/all_gather | solution.py:57
  75.8 11.1 %reduce-scatter.8.cloned.1.call-done = f32[16,48]{1,0:T(8,128)} async-done(((f32[64,48]{1,0:T(8,128)}), f32[16,48]{1,0:T(8,128)}) %reduce-scatter.8.cloned.1.call-update) | async-done | bytes 3088
  86.9 0.8 reshape.65
  87.7 0.1 copy.34
  87.8 9.1 %all_gather.26 = bf16[3,128,16]{2,1,0:T(8,128)(2,1)S(1)} all-gather(bf16[3,16,16]{2,1,0:T(8,128)(2,1)S(1)} %copy.34), channel_id=1, replica_groups=mesh['tgt'=8,'src'=4] {'tgt'}, dimensions={1}, use_global_device_ids=true | all-gather | bytes 13824 | tf_op jit(solution)/shard_map/all_gather | solution.py:76
  97.0 0.1 copy.30
  97.1 19.8 %fusion.16 = f32[1,3,16,64,1,1]{3,0,5,4,2,1:T(1,128)S(1)} fusion(bf16[3,128,16,1,1,1]{1,3,0,2,5,4:T(2,128)(2,1)S(1)} %copy.30, bf16[3,16,64,3,16,128]{5,4,3,2,1,0:T(8,128)(2,1)} %param.9), kind=kOutput, calls=%fused_computation.32 | convolution fusion | flops 37748736 | bytes 37773312 | tf_op jit(solution)/shard_map/xaqcbn,cnb->xaq/dot_general | solution.py:77
  116.8 0.1 copy.35
  117.0 0.7 reshape.66
  117.8 0.1 sub.195
  117.8 0.1 sub.205
  117.9 0.1 sub.200
  118.0 0.1 reshape.59
  118.1 0.1 sub.202
  118.2 0.1 sub.207
  118.2 0.1 sub.197
  118.3 0.6 dynamic-slice
  119.6 14.7 %reduce-scatter.10.cloned.1.call-done = f32[16,48]{1,0:T(8,128)} async-done(((f32[64,48]{1,0:T(8,128)}), f32[16,48]{1,0:T(8,128)}) %reduce-scatter.10.cloned.1.call-update) | async-done | bytes 3088
  134.3 0.8 reshape.67
  135.1 0.1 copy.36
  135.2 9.4 %all_gather.27 = f32[3,128,16]{2,1,0:T(8,128)S(1)} all-gather(f32[3,16,16]{2,1,0:T(8,128)S(1)} %copy.36), channel_id=1, replica_groups=mesh['tgt'=8,'src'=4] {'tgt'}, dimensions={1}, use_global_device_ids=true | all-gather | bytes 27648 | tf_op jit(solution)/shard_map/all_gather | solution.py:81
  144.6 0.1 mul.306
  144.7 0.1 mul.309
  144.8 0.1 mul.302
  144.8 5.6 %fusion.24 = (f32[512]{0:T(512)S(1)}, f32[512]{0:T(512)S(1)}, f32[512]{0:T(512)S(1)}) fusion(f32[2048]{0:T(1024)S(1)} %mul.302, f32[2048]{0:T(1024)S(1)} %sub.197, f32[512]{0:T(512)S(1)} %sub.195, f32[2048]{0:T(1024)S(1)} %sub.207, f32[512]{0:T(512)S(1)} %sub.205, f32[2048]{0:T(1024)S(1)} %sub.202, f32[512]{0:T(512)S(1)} %sub.200, f32[2048]{0:T(1024)S(1)} %mul.309, ...), kind=kLoop, calls=%fused_computation.50 | loop fusion | flops 32504320 | bytes 61440 | tf_op jit(solution)/shard_map/while/body/eval_jaxpr/reduce_sum | solution.py:25
  150.4 0.1 stack.44
  150.7 15.9 %all-reduce = f32[3,8,64]{2,1,0:T(8,128)S(1)} all-reduce(f32[3,8,64]{2,1,0:T(8,128)S(1)} %fusion.34), channel_id=5, replica_groups=mesh['tgt'=8,'src'=4] {'src'}, use_global_device_ids=true, to_apply=%region_5.0.clone | all-reduce | flops 1536 | bytes 12288
  166.6 0.6 constant_dynamic-slice_fusion.2
  (36 shorter events, 0.6 us)
Async XLA Ops:
  7.2 24.8 %copy-start = (f32[64,64]{1,0:T(8,128)S(1)}, f32[64,64]{1,0:T(8,128)}, u32[]{:S(2)}) copy-start(f32[64,64]{1,0:T(8,128)} %param.8) | copy-start | bytes 49156
  7.2 79.8 %reduce-scatter.8.cloned.1.call-start = ((), (), s32[]{:S(2)}) async-start(), calls=%async_computation.2 | async-start | bytes 40960
  56.5 11.0 %copy-start.1 = (f32[3,16,16]{2,1,0:T(8,128)S(1)}, f32[3,16,16]{2,1,0:T(8,128)}, u32[]{:S(2)}) copy-start(f32[3,16,16]{2,1,0:T(8,128)} %param.7) | copy-start | bytes 9220
  67.4 66.9 %reduce-scatter.10.cloned.1.call-start = ((), (), s32[]{:S(2)}) async-start(), calls=%async_computation.3 | async-start | bytes 40960
  97.1 21.3 %copy-start.3 = (u32[32]{0:T(128)S(1)}, u32[32]{0:T(128)}, u32[]{:S(2)}) copy-start(u32[32]{0:T(128)} %constant.79) | copy-start | bytes 388
  135.2 32.0 %copy-start.2 = (f32[3,16,16]{2,1,0:T(8,128)}, f32[3,16,16]{2,1,0:T(8,128)S(1)}, u32[]{:S(2)}) copy-start(f32[3,16,16]{2,1,0:T(8,128)S(1)} %copy.36) | copy-start | bytes 9220
Sparse Core Ops, SparseCore 0:
  67.5 19.3 reduce-scatter.7
  117.8 16.4 reduce-scatter.9
where the time goes:
time: 174 us
  blocking collectives  89.2 us (51%)
  waiting for transfers between devices  25.9 us (15%)
  matrix products  20.6 us (12%)
  other arithmetic  15.1 us (9%)
  between operations  14.8 us (9%)
  local copies, waits for them, and re-layouts  8.12 us (5%)
    unnamed x4, waiting for transfers between devices  25.9 us
    dot_general x1, matrix products, per_device(): jnp.einsum('xaqcbn,cnb->xaq', shell_inverse, columns, preferred_element_t...  19.8 us
    unnamed x1, blocking collectives  15.9 us
    reduce_sum x3, other arithmetic, stokes_flow(): jnp.sum(diagonal_part * strength[0][None, :] + projection * delta_x, axis=1)  15 us
    all_gather x1, blocking collectives, per_device(): fibre_block = lax.all_gather(fibre_points, 'src', axis=1, tiled=True)  14.9 us
    all_gather x1, blocking collectives, per_device(): shell_rows = lax.all_gather(shell_points, 'src', axis=2, tiled=True)  13.3 us
    all_gather x1, blocking collectives, per_device(): column_density = lax.all_gather(density, 'tgt', axis=1, tiled=True)  9.42 us
    all_gather x1, blocking collectives, per_device(): lax.all_gather(shell_flow.astype(jnp.bfloat16), 'tgt', axis=1, tiled=True)  9.14 us
  transfers between devices with their start and end apart: 2, of which 2 were waited for; matrix products, arithmetic and copies ran while one was open for 1% of the time, Pallas kernels for 0%

commit v1 on v0

v1 whole, which is shorter than its diff:
```python
import functools
import math

import jax
import jax.numpy as jnp
from jax import lax
from jax.experimental import pallas as pl
from jax.experimental.pallas import tpu as pltpu
from jax.sharding import PartitionSpec as P

mobility = 1.0 / (8.0 * math.pi)
soften_sq = 0.0025
LANES = 128
SUB = 8
HIGHEST = lax.Precision.HIGHEST
MESH = pl.DeviceIdType.MESH
f32 = jnp.float32


def iotas(rows=SUB):
    lane = lax.broadcasted_iota(jnp.int32, (rows, LANES), 1)
    sub = lax.broadcasted_iota(jnp.int32, (rows, LANES), 0)
    return lane, sub


def flow(src_ref, start, count, targets, accs, unroll):
    unroll = math.gcd(unroll, count)

    def body(i, accs):
        accs = list(accs)
        for u in range(unroll):
            j = start + i * unroll + u
            sx, sy, sz, gx, gy, gz = [src_ref[j, c] for c in range(6)]
            for g, (tx, ty, tz) in enumerate(targets):
                dx, dy, dz = tx - sx, ty - sy, tz - sz
                q = dx * dx + dy * dy + (dz * dz + soften_sq)
                inv = lax.rsqrt(q)
                cubed = inv * inv * inv
                proj = (dx * gx + dy * gy + dz * gz) * cubed
                diag = (q + soften_sq) * cubed
                accs[3 * g] += diag * gx + proj * dx
                accs[3 * g + 1] += diag * gy + proj * dy
                accs[3 * g + 2] += diag * gz + proj * dz
        return tuple(accs)

    return lax.fori_loop(0, count // unroll, body, tuple(accs))


def fold_rows(rows, sub):
    def step(a, b, width):
        low = (sub & width) == 0
        up = a + pltpu.roll(a, SUB - width, 0)
        down = b + pltpu.roll(b, width, 0)
        return jnp.where(low, up, down)

    width = 4
    level = rows
    half = len(rows) // 2
    while half >= 1:
        level = [step(level[i], level[i + half], width) for i in range(half)]
        width //= 2
        half //= 2
    return level[0]


def kernel(
    nt, ns, fib_ref, shell_ref, bend_ref, mat_ref, vel_ref, den_ref,
    mat, gbuf, pbuf, dbuf, cbuf, part, rbuf, tbs, tbf, wide, src1, src2, fib_acc, weave,
    posblk, denblk, colblk, ptblk, lane_ref,
    mat_sem, g_send, g_recv, p_send, p_recv, c_send, c_recv, r_send, r_recv, d_send, d_recv,
):
    t, s = lax.axis_index("tgt"), lax.axis_index("src")
    n_dev = nt * ns
    al, ql = shell_ref.shape[1], shell_ref.shape[2]
    fl, nodes = fib_ref.shape[1], fib_ref.shape[2]
    fib_groups = LANES // SUB
    qv = min(ql, LANES // al)
    nvec = ql // qv
    lane_ref[...] = iotas(ql)[0]
    sub = iotas()[1]
    sub16 = iotas(ql)[1]
    lane, lane16 = lane_ref[pl.ds(0, SUB), :], lane_ref[...]

    def fetch(k):
        to = lax.rem(s + 1 + k, ns)
        return pltpu.make_async_copy(
            mat_ref.at[:, :, pl.ds(to * ql, ql)], mat.at[k], mat_sem.at[k]
        )

    for k in range(ns):
        fetch(k).start()

    def peer(i):
        return {"tgt": lax.rem(t + lax.rem(i, nt), nt), "src": lax.rem(s + i // nt, ns)}

    gbuf[...] = jnp.zeros_like(gbuf)
    barrier = pltpu.get_barrier_semaphore()

    def greet(i, _):
        pl.semaphore_signal(barrier, inc=1, device_id=peer(i), device_id_type=MESH)
        return 0

    lax.fori_loop(1, n_dev, greet, 0)

    ptblk[...] = jnp.zeros_like(ptblk)
    posblk[...] = jnp.zeros_like(posblk)
    denblk[...] = jnp.zeros_like(denblk)
    points = jnp.concatenate([fib_ref[:, f, :] for f in range(fl)], axis=1)
    ptblk[pl.ds(0, 3), :] = points
    bend = bend_ref[...]
    blank = jnp.zeros_like(bend)
    weave[...] = jnp.concatenate(
        [
            jnp.concatenate([bend if i == j else blank for j in range(fl)], axis=1)
            for i in range(fl)
        ],
        axis=0,
    )

    def spread(a, reps):
        out = []
        for c in range(3):
            row = shell_ref[c, pl.ds(a, 1), :]
            eye = lax.broadcasted_iota(jnp.int32, (ql, ql), 0) == lax.broadcasted_iota(
                jnp.int32, (ql, ql), 1
            )
            col = jnp.sum(jnp.where(eye, 1.0, 0.0) * row, axis=1, keepdims=True)
            wide_col = jnp.broadcast_to(col, (ql, LANES))
            tbs[a, c] = wide_col
            out.append(jnp.where(lax.rem(lane16, al) == a, wide_col, reps[c]))
        return tuple(out)

    reps = lax.fori_loop(0, al, spread, tuple(jnp.zeros((ql, LANES), f32) for _ in range(3)))

    def weave_rows(block, values):
        for c in range(3):
            for h in range(nvec):
                piece = values[c][h * qv:(h + 1) * qv]
                hit = lax.div(lane16[:qv], al) == sub16[:qv]
                block[pl.ds(c * nvec + h, 1), :] = jnp.sum(
                    jnp.where(hit, piece, 0.0), axis=0, keepdims=True
                )

    weave_rows(posblk, reps)

    def spread_fibre(g, _):
        for c in range(3):
            row = ptblk[pl.ds(c, 1), :]
            hit = jnp.where(lane == sub + g * SUB, 1.0, 0.0)
            col = jnp.sum(hit * row, axis=1, keepdims=True)
            tbf[g, c] = jnp.broadcast_to(col, (SUB, LANES))
        return 0

    lax.fori_loop(0, fib_groups, spread_fibre, 0)

    me = s * nt + t
    gbuf[me] = ptblk[...]
    pbuf[me] = posblk[...]
    pl.semaphore_wait(barrier, n_dev - 1)

    def spread_out(block, buf, rows, send, recv):
        def one(i, _):
            pltpu.make_async_remote_copy(
                src_ref=block.at[pl.ds(0, rows)],
                dst_ref=buf.at[me, pl.ds(0, rows)],
                send_sem=send,
                recv_sem=recv.at[s],
                device_id=peer(i),
                device_id_type=MESH,
            ).start()
            return 0

        lax.fori_loop(1, n_dev, one, 0)

    def arrived(buf, rows, recv, k):
        frm = lax.rem(s + k, ns)
        ref = buf.at[pl.ds(0, nt if k else nt - 1), pl.ds(0, rows)]
        pltpu.make_async_copy(ref, ref, recv.at[frm]).wait()

    def sent(buf, rows, send):
        ref = buf.at[pl.ds(0, n_dev - 1), pl.ds(0, rows)]
        pltpu.make_async_copy(ref, ref, send).wait()

    spread_out(ptblk, gbuf, 3, g_send, g_recv)
    spread_out(posblk, pbuf, SUB, p_send, p_recv)
    for k in range(ns):
        arrived(gbuf, 3, g_recv, k)

    all_points = gbuf[...].reshape(n_dev * SUB, LANES)
    wide[...] = (
        lax.dot_general(
            all_points, weave[...], (((1,), (1,)), ((), ())),
            precision=HIGHEST, preferred_element_type=f32,
        )
        * (-mobility)
    ).reshape(n_dev, SUB, LANES)

    def plane(j, _):
        for c in range(3):
            src1[j, c] = jnp.broadcast_to(gbuf[j, pl.ds(c, 1), :], (SUB, LANES))
            src1[j, c + 3] = jnp.broadcast_to(wide[j, pl.ds(c, 1), :], (SUB, LANES))
        return 0

    lax.fori_loop(0, n_dev, plane, 0)
    halves = ql // SUB
    zero = jnp.zeros((SUB, LANES), f32)

    def shell_targets(a, cols):
        groups = [
            tuple(tbs[a, c, pl.ds(h * SUB, SUB), :] for c in range(3)) for h in range(halves)
        ]
        accs = flow(src1, 0, n_dev, groups, [zero] * (3 * halves), 4)
        here = lane == t * al + a
        return tuple(
            jnp.where(here, jnp.sum(accs[i], axis=1, keepdims=True), cols[i])
            for i in range(3 * halves)
        )

    cols = lax.fori_loop(0, al, shell_targets, tuple([zero] * (3 * halves)))
    for c in range(3):
        colblk[c] = jnp.concatenate(
            [cols[3 * h + c] for h in range(halves)], axis=0
        ).astype(jnp.bfloat16)
    cbuf[t] = colblk[...]

    def send_cols(i, _):
        pltpu.make_async_remote_copy(
            src_ref=colblk, dst_ref=cbuf.at[t], send_sem=c_send, recv_sem=c_recv,
            device_id={"tgt": lax.rem(t + i, nt), "src": s}, device_id_type=MESH,
        ).start()
        return 0

    lax.fori_loop(1, nt, send_cols, 0)

    def fibre_targets(src_ref, start, count, first):
        def one(i, _):
            groups = [tuple(tbf[2 * i + h, c] for c in range(3)) for h in range(2)]
            accs = [
                zero if first else fib_acc[2 * i + h, c] for h in range(2) for c in range(3)
            ]
            accs = flow(src_ref, start, count, groups, accs, 4)
            for h in range(2):
                for c in range(3):
                    fib_acc[2 * i + h, c] = accs[3 * h + c]
            return 0

        lax.fori_loop(0, fib_groups // 2, one, 0)

    fibre_targets(src1, 0, n_dev, True)

    others = cbuf.at[pl.ds(0, nt - 1)]
    pltpu.make_async_copy(others, others, c_recv).wait()
    v = lax.fori_loop(
        0, nt, lambda i, total: total + cbuf[i].astype(f32), jnp.zeros(cbuf.shape[1:], f32)
    )

    def send_part(k):
        to = lax.rem(s + 1 + k, ns)
        return pltpu.make_async_remote_copy(
            src_ref=part.at[k], dst_ref=rbuf.at[k],
            send_sem=r_send.at[k], recv_sem=r_recv.at[k],
            device_id={"tgt": t, "src": to}, device_id_type=MESH,
        )

    def place(a, folded, dens):
        here = lax.rem(lane, al) == a
        return tuple(
            jnp.where(here, jnp.sum(y, axis=1, keepdims=True), d) for y, d in zip(folded, dens)
        )

    for k in range(ns):
        fetch(k).wait()

        def row_block(a, carry):
            folded, dens = carry
            dens = place(a - 1, folded, dens)
            new = []
            for x in range(3):
                for h in range(halves):
                    rows = []
                    for r in range(SUB):
                        prod = mat[k, x, a, h * SUB + r].astype(f32) * v
                        both = prod[0] + prod[1] + prod[2]
                        rows.append(
                            sum(both[i * SUB:(i + 1) * SUB] for i in range(halves))
                        )
                    new.append(fold_rows(rows, sub))
            return tuple(new), dens

        empty = tuple([zero] * (3 * halves))
        folded, dens = lax.fori_loop(0, al, row_block, (empty, empty))
        dens = place(al - 1, folded, dens)
        for x in range(3):
            for h in range(halves):
                part[k, x, pl.ds(h * SUB, SUB), :] = dens[x * halves + h]
        if k < ns - 1:
            send_part(k).start()

    total = part[ns - 1]
    for k in range(ns - 1):
        send_part(k).wait_recv()
        total = total + rbuf[k]
    total = -total
    weave_rows(denblk, [total[x] for x in range(3)])
    dbuf[me] = denblk[...]
    spread_out(denblk, dbuf, SUB, d_send, d_recv)

    pick = max(al, SUB)
    pl_lane, pl_sub = iotas(pick)
    eye = jnp.where(pl_lane == pl_sub, 1.0, 0.0).astype(f32)
    for x in range(3):
        den_ref[x] = lax.dot_general(
            eye, total[x], (((1,), (1,)), ((), ())), precision=HIGHEST, preferred_element_type=f32
        )[:al]

    for k in range(ns):
        arrived(pbuf, SUB, p_recv, k)
        arrived(dbuf, SUB, d_recv, k)
        base = lax.rem(s + k, ns) * nt

        def plane_back(j, _):
            for h in range(nvec):
                for c in range(3):
                    r = pl.ds(c * nvec + h, 1)
                    src2[j * nvec + h, c] = jnp.broadcast_to(pbuf[base + j, r, :], (SUB, LANES))
                    src2[j * nvec + h, c + 3] = jnp.broadcast_to(
                        dbuf[base + j, r, :] * mobility, (SUB, LANES)
                    )
            return 0

        lax.fori_loop(0, nt, plane_back, 0)
        fibre_targets(src2, 0, nt * nvec, False)

    def gather_rows(g, rows):
        hit = lane == sub + g * SUB
        return tuple(
            rows[c] + jnp.where(hit, jnp.sum(fib_acc[g, c], axis=1, keepdims=True), 0.0)
            for c in range(3)
        )

    rows = lax.fori_loop(0, fib_groups, gather_rows, (zero,) * 3)
    for c in range(3):
        row = jnp.sum(rows[c], axis=0, keepdims=True)
        for f in range(fl):
            vel_ref[c, pl.ds(f, 1), :] = row[:, f * nodes:(f + 1) * nodes]

    sent(gbuf, 3, g_send)
    sent(pbuf, SUB, p_send)
    sent(dbuf, SUB, d_send)
    pltpu.make_async_copy(others, others, c_send).wait()
    for k in range(ns - 1):
        send_part(k).wait_send()


def per_device(nt, ns, fibre_points, shell_points, bending, shell_inverse):
    n_dev = nt * ns
    _, al, ql = shell_points.shape
    fib_groups = LANES // SUB
    nvec = ql // min(ql, LANES // al)
    vmem = pl.BlockSpec(memory_space=pltpu.VMEM)
    dma = pltpu.SemaphoreType.DMA
    block = shell_inverse.shape
    return pl.pallas_call(
        functools.partial(kernel, nt, ns),
        out_shape=(
            jax.ShapeDtypeStruct(fibre_points.shape, f32),
            jax.ShapeDtypeStruct(shell_points.shape, f32),
        ),
        in_specs=[vmem, vmem, vmem, pl.BlockSpec(memory_space=pltpu.HBM)],
        out_specs=(vmem, vmem),
        scratch_shapes=[
            pltpu.VMEM((ns, 3, al, ql) + block[3:], jnp.bfloat16),
            pltpu.VMEM((n_dev, SUB, LANES), f32),
            pltpu.VMEM((n_dev, SUB, LANES), f32),
            pltpu.VMEM((n_dev, SUB, LANES), f32),
            pltpu.VMEM((nt,) + block[3:], jnp.bfloat16),
            pltpu.VMEM((ns, 3, ql, LANES), f32),
            pltpu.VMEM((ns, 3, ql, LANES), f32),
            pltpu.VMEM((al, 3, ql, LANES), f32),
            pltpu.VMEM((fib_groups, 3, SUB, LANES), f32),
            pltpu.VMEM((n_dev, SUB, LANES), f32),
            pltpu.VMEM((n_dev, 6, SUB, LANES), f32),
            pltpu.VMEM((nt * nvec, 6, SUB, LANES), f32),
            pltpu.VMEM((fib_groups, 3, SUB, LANES), f32),
            pltpu.VMEM((LANES, LANES), f32),
            pltpu.VMEM((SUB, LANES), f32),
            pltpu.VMEM((SUB, LANES), f32),
            pltpu.VMEM(block[3:], jnp.bfloat16),
            pltpu.VMEM((SUB, LANES), f32),
            pltpu.VMEM((ql, LANES), jnp.int32),
            dma((ns,)), dma, dma((ns,)), dma, dma((ns,)), dma, dma, dma((ns,)), dma((ns,)),
            dma, dma((ns,)),
        ],
        compiler_params=pltpu.CompilerParams(
            collective_id=0, has_side_effects=True, vmem_limit_bytes=60 * 1024 * 1024
        ),
        name="shell_step",
    )(fibre_points, shell_points, bending, shell_inverse)


def solution(mesh):
    placed = (
        P(None, ("tgt", "src"), None),
        P(None, "tgt", "src"),
        P(),
        P(None, "tgt", None, None, "src", None),
    )
    return jax.shard_map(
        functools.partial(per_device, mesh.shape["tgt"], mesh.shape["src"]),
        mesh=mesh,
        in_specs=placed,
        out_specs=(P(None, ("tgt", "src"), None), P(None, "tgt", "src")),
        check_vma=False,
    )
```

time: 174 us -> 48.2 us (0.28)
  blocking collectives: 89.2 us -> 0 us
  Pallas kernels: 0 us -> 44.7 us
  waiting for transfers between devices: 25.9 us -> 0 us
  matrix products: 20.6 us -> 0 us
  other arithmetic: 15.1 us -> 0 us
  between operations: 14.8 us -> 0.64 us
  local copies, waits for them, and re-layouts: 8.12 us -> 2.6 us
    all_gather x7 -> x0, blocking collectives: 73.3 us -> none  [the longest x1 14.9 us: per_device(): fibre_block = lax.all_gather(fibre_points, 'src', axis=1, tiled=True)]
    pallas_call x0 -> x1, Pallas kernels: none -> 44.7 us  [per_device(): pl.pallas_call(functools.partial(kernel, nt, ns), out_shape=(jax.ShapeDty...]
    unnamed x4 -> x0, waiting for transfers between devices: 25.9 us -> none
    dot_general x2 -> x0, matrix products: 20.6 us -> none  [the longest x1 19.8 us: per_device(): jnp.einsum('xaqcbn,cnb->xaq', shell_inverse, columns, preferred_element_t...]
    unnamed x1 -> x0, blocking collectives: 15.9 us -> none
    reduce_sum x3 -> x0, other arithmetic: 15 us -> none  [stokes_flow(): jnp.sum(diagonal_part * strength[0][None, :] + projection * delta_x, axis=1)]
    unnamed x20 -> x2, local copies, waits for them, and re-layouts: 6.08 us -> 2.6 us
  transfers between devices with their start and end apart: 2 -> 0, of which waited for: 2 -> 0; matrix products, arithmetic and copies ran while one was open for 1% -> 0% of each run, Pallas kernels for 0% -> 0%
where the time goes in v1:
time: 48.2 us; the launch traced here: 47.9 us
  Pallas kernels  44.7 us (93%)
  local copies, waits for them, and re-layouts  2.6 us (5%)
  between operations  0.64 us (1%)
    pallas_call x1, Pallas kernels, per_device(): pl.pallas_call(functools.partial(kernel, nt, ns), out_shape=(jax.ShapeDty...  44.7 us
    unnamed x2, local copies, waits for them, and re-layouts  2.6 us

profile of v1, /device:TPU:0, one launch (start us, length us, event | category | flops | bytes accessed | tf_op | source)
XLA Modules:
  0.0 47.9 jit_solution(15102932403019410702)
XLA Ops:
  0.6 44.7 %shell_step.1 = (f32[3,2,64]{2,1,0:T(2,128)}, f32[3,16,16]{2,1,0:T(8,128)}) custom-call(f32[3,2,64]{2,1,0:T(2,128)} %fib_ref.1, f32[3,16,16]{2,1,0:T(8,128)} %shell_ref.1, f32[64,64]{1,0:T(8,128)} %bend_ref.1, bf16[3,16,64,3,16,128]{5,4,3,2,1,0:T(8,128)(2,1)} %mat_ref.1), custom_call_target="tpu_custom_call" | custom-call | tf_op jit(solution)/shard_map/shell_step/pallas_call | solution.py:363
  45.3 1.3 %copy.8 = f32[3,2,64]{2,1,0:T(2,128)} copy(f32[3,2,64]{2,1,0:T(2,128)} %get-tuple-element.4) | data formatting | bytes 3072
  46.6 1.3 %copy.9 = f32[3,16,16]{2,1,0:T(8,128)} copy(f32[3,16,16]{2,1,0:T(8,128)} %get-tuple-element.5) | data formatting | bytes 6144

commit v2 on v1

--- a/solution.py
+++ b/solution.py
@@ -209,7 +209,7 @@
         groups = [
             tuple(tbs[a, c, pl.ds(h * SUB, SUB), :] for c in range(3)) for h in range(halves)
         ]
-        accs = flow(src1, 0, n_dev, groups, [zero] * (3 * halves), 4)
+        accs = flow(src1, 0, n_dev, groups, [zero] * (3 * halves), 16)
         here = lane == t * al + a
         return tuple(
             jnp.where(here, jnp.sum(accs[i], axis=1, keepdims=True), cols[i])
@@ -238,7 +238,7 @@
             accs = [
                 zero if first else fib_acc[2 * i + h, c] for h in range(2) for c in range(3)
             ]
-            accs = flow(src_ref, start, count, groups, accs, 4)
+            accs = flow(src_ref, start, count, groups, accs, 16)
             for h in range(2):
                 for c in range(3):
                     fib_acc[2 * i + h, c] = accs[3 * h + c]

time: 48.2 us -> 46.8 us (0.971)
  Pallas kernels: 44.7 us -> 43.3 us
    pallas_call x1, Pallas kernels: 44.7 us -> 43.3 us  [per_device(): pl.pallas_call(functools.partial(kernel, nt, ns), out_shape=(jax.ShapeDty...]
where the time goes in v2:
time: 46.8 us; the launch traced here: 46.5 us
  Pallas kernels  43.3 us (93%)
  local copies, waits for them, and re-layouts  2.6 us (6%)
  between operations  0.64 us (1%)
    pallas_call x1, Pallas kernels, per_device(): pl.pallas_call(functools.partial(kernel, nt, ns), out_shape=(jax.ShapeDty...  43.3 us
    unnamed x2, local copies, waits for them, and re-layouts  2.6 us

profile of v2, /device:TPU:0, one launch (start us, length us, event | category | flops | bytes accessed | tf_op | source)
XLA Modules:
  0.0 46.5 jit_solution(17190189038587427568)
XLA Ops:
  0.6 43.3 %shell_step.1 = (f32[3,2,64]{2,1,0:T(2,128)}, f32[3,16,16]{2,1,0:T(8,128)}) custom-call(f32[3,2,64]{2,1,0:T(2,128)} %fib_ref.1, f32[3,16,16]{2,1,0:T(8,128)} %shell_ref.1, f32[64,64]{1,0:T(8,128)} %bend_ref.1, bf16[3,16,64,3,16,128]{5,4,3,2,1,0:T(8,128)(2,1)} %mat_ref.1), custom_call_target="tpu_custom_call" | custom-call | tf_op jit(solution)/shard_map/shell_step/pallas_call | solution.py:363
  43.9 1.3 %copy.8 = f32[3,2,64]{2,1,0:T(2,128)} copy(f32[3,2,64]{2,1,0:T(2,128)} %get-tuple-element.4) | data formatting | bytes 3072
  45.2 1.3 %copy.9 = f32[3,16,16]{2,1,0:T(8,128)} copy(f32[3,16,16]{2,1,0:T(8,128)} %get-tuple-element.5) | data formatting | bytes 6144
